TPU v7x, 256 devices: a whole 4x4x8 slice. The times are simulated.
256 devices in a mesh: blk: 64 (over x, z, y_hi), dp: 4 (over y_lo, core).
Axes of the slice: x: 4, y: 4 (y_hi: 2, y_lo: 2; y = y_hi * 2 + y_lo), z: 8, core: 2. Of those that a mesh axis runs over, the one named last changes fastest.
Arguments:
- images: bfloat16 [32768, 768], P(('dp', 'blk')), parts along dimension 0, may hold values from -4 to 4
- texts: bfloat16 [32768, 768], P(('dp', 'blk')), parts along dimension 0, may hold values from -4 to 4
- scale: float32 [1], replicated, may hold values from 10 to 20
- cotangent: float32 [2, 32768], P(None, ('dp', 'blk')), parts along dimension 1, may hold values from 0.5 to 2
Outputs:
- row_losses: float32 [2, 32768], P(None, ('dp', 'blk')), parts along dimension 1
- grad_images: float32 [32768, 768], P(('dp', 'blk')), parts along dimension 0
- grad_texts: float32 [32768, 768], P(('dp', 'blk')), parts along dimension 0
There are 4 independent parts, one for each index of `dp`. A program takes and returns all parts, laid end to end along the dimension named above; an argument that names none is the same for every part. Nothing has to cross between parts.
All inputs are finite; a program needn't handle non-finite values.
Results may differ from a plain program's by a relative error of at most 0.0019.
Values may be sent and summed in bfloat16 or wider, within the bound.
No kernel may reach another device: no remote copies, remote signals or barrier semaphores. Data moves between devices by JAX's collectives and lax.ppermute only.
A program may use at most 64 MiB of HBM per device.

v0:
```python
import jax
import jax.numpy as jnp
from jax import lax
from jax.sharding import PartitionSpec as P

GROUP = 8


def shifted(value, axis, steps):
    count = lax.axis_size(axis)
    pairs = [(source, (source + steps) % count) for source in range(count)]
    return lax.ppermute(value, axis, pairs)


def dot_rows(left, right):
    return lax.dot_general(
        left, right, (((1,), (1,)), ((), ())), preferred_element_type=jnp.float32
    )


def dot_lead(left, right):
    return lax.dot_general(
        left, right, (((0,), (0,)), ((), ())), preferred_element_type=jnp.float32
    )


def merge_pair(first, second):
    max_new = jnp.maximum(first[0], second[0])
    return (
        max_new,
        first[1] * jnp.exp(first[0] - max_new) + second[1] * jnp.exp(second[0] - max_new),
    )


def block_stats(scores, along):
    top_value = jnp.max(scores, axis=along)
    total_sum = jnp.sum(jnp.exp(scores - jnp.expand_dims(top_value, along)), axis=along)
    return (top_value, total_sum)


def shards(images, texts, scale, cotangent):
    row_count = images.shape[0]
    logit_scale = scale[0]
    cot_rows = cotangent[0]
    cot_cols = cotangent[1]
    cycle_size = lax.axis_size("blk")
    span_count = cycle_size // GROUP
    image_pieces = [images] + [shifted(images, "blk", -k) for k in range(1, GROUP)]
    text_pieces = [texts] + [shifted(texts, "blk", -GROUP * m) for m in range(1, span_count)]
    text_window = jnp.concatenate(text_pieces, axis=0)
    col_part = (
        jnp.full((span_count * row_count,), -1e30, jnp.float32),
        jnp.zeros((span_count * row_count,), jnp.float32),
    )
    row_parts = []
    for image_block in image_pieces:
        scores = logit_scale * dot_rows(text_window, image_block)
        row_parts.append(block_stats(scores, 0))
        col_part = merge_pair(col_part, block_stats(scores, 1))
    row_part = row_parts[0]
    for k in range(1, GROUP):
        row_part = merge_pair(row_part, shifted(row_parts[k], "blk", k))
    col_own = (col_part[0][:row_count], col_part[1][:row_count])
    for m in range(1, span_count):
        sent = (
            col_part[0][m * row_count : (m + 1) * row_count],
            col_part[1][m * row_count : (m + 1) * row_count],
        )
        col_own = merge_pair(col_own, shifted((sent[0], sent[1]), "blk", GROUP * m))
    row_lse = row_part[0] + jnp.log(row_part[1])
    col_lse = col_own[0] + jnp.log(col_own[1])
    matched = logit_scale * jnp.sum(images.astype(jnp.float32) * texts.astype(jnp.float32), axis=1)
    row_losses = jnp.stack([row_lse - matched, col_lse - matched])
    row_stats = [(row_lse, cot_rows)] + [
        shifted((row_lse, cot_rows), "blk", -k) for k in range(1, GROUP)
    ]
    col_stats = [(col_lse, cot_cols)] + [
        shifted((col_lse, cot_cols), "blk", -GROUP * m) for m in range(1, span_count)
    ]
    col_lse_win = jnp.concatenate([piece[0] for piece in col_stats], axis=0)
    col_cot_win = jnp.concatenate([piece[1] for piece in col_stats], axis=0)
    acc_texts = jnp.zeros((span_count * row_count, images.shape[1]), jnp.float32)
    image_terms = None
    for k, image_block in enumerate(image_pieces):
        scores = logit_scale * dot_rows(text_window, image_block)
        weights = row_stats[k][1][None, :] * jnp.exp(
            scores - row_stats[k][0][None, :]
        ) + col_cot_win[:, None] * jnp.exp(scores - col_lse_win[:, None])
        weights_low = weights.astype(jnp.bfloat16)
        partial_value = dot_lead(weights_low, text_window)
        acc_texts = acc_texts + jnp.dot(
            weights_low, image_block, preferred_element_type=jnp.float32
        )
        if k == 0:
            image_terms = partial_value
        else:
            image_terms = image_terms + shifted(partial_value, "blk", k)
    text_terms = acc_texts[:row_count]
    for m in range(1, span_count):
        text_terms = text_terms + shifted(
            acc_texts[m * row_count : (m + 1) * row_count], "blk", GROUP * m
        )
    both_cot = (cot_rows + cot_cols)[:, None]
    grad_images = logit_scale * (image_terms - both_cot * texts.astype(jnp.float32))
    grad_texts = logit_scale * (text_terms - both_cot * images.astype(jnp.float32))
    return (row_losses, grad_images, grad_texts)


def solution(mesh):
    return jax.shard_map(
        shards,
        mesh=mesh,
        in_specs=(P(("dp", "blk"), None), P(("dp", "blk"), None), P(), P(None, ("dp", "blk"))),
        out_specs=(P(None, ("dp", "blk")), P(("dp", "blk"), None), P(("dp", "blk"), None)),
        check_vma=False,
    )
```

profile of v0, /device:TPU:64, one launch (start us, length us, event | category | flops | bytes accessed | tf_op | source)
XLA Modules:
  0.0 501.8 jit_solution(12225414257575266772)
XLA Ops:
  1.9 5.4 %collective-permute-start.48 = (f32[128]{0:T(128)}, f32[128]{0:T(128)}, u32[]{:S(2)}, u32[]{:S(2)}) collective-permute-start(f32[128]{0:T(128)} %get-tuple-element.64), channel_id=1, source_target_pairs={{0,32},{4,36},{8,40},{12,44},{16,48},{20,52},{24,56},{28,60},{32,6... | collective-permute-start | bytes 1544 | tf_op jit(solution)/shard_map/ppermute | solution.py:12
  12.9 6.0 %collective-permute-start.42 = (f32[128]{0:T(128)}, f32[128]{0:T(128)S(1)}, u32[]{:S(2)}, u32[]{:S(2)}) collective-permute-start(f32[128]{0:T(128)} %get-tuple-element.64), channel_id=1, source_target_pairs={{0,224},{4,228},{8,232},{12,236},{16,240},{20,244},{24,248},{28,25... | collective-permute-start | bytes 1544 | tf_op jit(solution)/shard_map/ppermute | solution.py:12
  26.7 5.4 %collective-permute-start.44 = (f32[128]{0:T(128)}, f32[128]{0:T(128)S(1)}, u32[]{:S(2)}, u32[]{:S(2)}) collective-permute-start(f32[128]{0:T(128)} %get-tuple-element.64), channel_id=1, source_target_pairs={{0,160},{4,164},{8,168},{12,172},{16,176},{20,180},{24,184},{28,18... | collective-permute-start | bytes 1544 | tf_op jit(solution)/shard_map/ppermute | solution.py:12
  35.2 5.4 %collective-permute-start.6 = (bf16[128,768]{1,0:T(8,128)(2,1)}, bf16[128,768]{1,0:T(8,128)(2,1)S(1)}, u32[]{:S(2)}, u32[]{:S(2)}) collective-permute-start(bf16[128,768]{1,0:T(8,128)(2,1)} %param.5), channel_id=1, source_target_pairs={{0,32},{4,36},{8,40},{12,44},{16,48},{20,52},{24,56},{28,60},{32,6... | collective-permute-start | bytes 589832 | tf_op jit(solution)/shard_map/ppermute | solution.py:12
  46.3 9.3 %collective-permute-done = bf16[128,768]{1,0:T(8,128)(2,1)S(1)} collective-permute-done((bf16[128,768]{1,0:T(8,128)(2,1)}, bf16[128,768]{1,0:T(8,128)(2,1)S(1)}, u32[]{:S(2)}, u32[]{:S(2)}) %collective-permute-start) | collective-permute-done | bytes 196640 | tf_op jit(solution)/shard_map/ppermute | solution.py:12
  55.6 7.8 %collective-permute-start.2 = (bf16[128,768]{1,0:T(8,128)(2,1)}, bf16[128,768]{1,0:T(8,128)(2,1)S(1)}, u32[]{:S(2)}, u32[]{:S(2)}) collective-permute-start(bf16[128,768]{1,0:T(8,128)(2,1)} %param.5), channel_id=1, source_target_pairs={{0,160},{4,164},{8,168},{12,172},{16,176},{20,180},{24,184},{28,18... | collective-permute-start | bytes 589832 | tf_op jit(solution)/shard_map/ppermute | solution.py:12
  67.6 13.5 %collective-permute-start.4 = (bf16[128,768]{1,0:T(8,128)(2,1)S(1)}, bf16[128,768]{1,0:T(8,128)(2,1)S(1)}, u32[]{:S(2)}, u32[]{:S(2)}) collective-permute-start(bf16[128,768]{1,0:T(8,128)(2,1)S(1)} %copy-done.3), channel_id=1, source_target_pairs={{0,96},{4,100},{8,104},{12,108},{16,112},{20,116},{24,120},{28,124... | collective-permute-start | bytes 589832 | tf_op jit(solution)/shard_map/ppermute | solution.py:12
  85.8 6.7 %collective-permute-start.15 = (bf16[128,768]{1,0:T(8,128)(2,1)S(1)}, bf16[128,768]{1,0:T(8,128)(2,1)S(1)}, u32[]{:S(2)}, u32[]{:S(2)}) collective-permute-start(bf16[128,768]{1,0:T(8,128)(2,1)S(1)} %copy-done.2), channel_id=1, source_target_pairs={{0,236},{4,240},{8,244},{12,248},{16,252},{20,0},{24,4},{28,8},{32... | collective-permute-start | bytes 589832 | tf_op jit(solution)/shard_map/ppermute | solution.py:12
  92.5 4.8 collective-permute-start.13
  99.4 5.3 %collective-permute-start.11 = (bf16[128,768]{1,0:T(8,128)(2,1)S(1)}, bf16[128,768]{1,0:T(8,128)(2,1)S(1)}, u32[]{:S(2)}, u32[]{:S(2)}) collective-permute-start(bf16[128,768]{1,0:T(8,128)(2,1)S(1)} %copy-done.2), channel_id=1, source_target_pairs={{0,244},{4,248},{8,252},{12,0},{16,4},{20,8},{24,12},{28,16},{32,2... | collective-permute-start | bytes 589832 | tf_op jit(solution)/shard_map/ppermute | solution.py:12
  105.3 7.0 %collective-permute-done.17 = bf16[128,768]{1,0:T(8,128)(2,1)S(1)} collective-permute-done((bf16[128,768]{1,0:T(8,128)(2,1)S(1)}, bf16[128,768]{1,0:T(8,128)(2,1)S(1)}, u32[]{:S(2)}, u32[]{:S(2)}) %collective-permute-start.17) | collective-permute-done | bytes 196640 | tf_op jit(solution)/shard_map/ppermute | solution.py:12
  113.5 7.4 %collective-permute-done.15 = bf16[128,768]{1,0:T(8,128)(2,1)S(1)} collective-permute-done((bf16[128,768]{1,0:T(8,128)(2,1)S(1)}, bf16[128,768]{1,0:T(8,128)(2,1)S(1)}, u32[]{:S(2)}, u32[]{:S(2)}) %collective-permute-start.15) | collective-permute-done | bytes 196640 | tf_op jit(solution)/shard_map/ppermute | solution.py:12
  121.0 5.4 %collective-permute-start.7 = (bf16[128,768]{1,0:T(8,128)(2,1)S(1)}, bf16[128,768]{1,0:T(8,128)(2,1)S(1)}, u32[]{:S(2)}, u32[]{:S(2)}) collective-permute-start(bf16[128,768]{1,0:T(8,128)(2,1)S(1)} %copy-done.2), channel_id=1, source_target_pairs={{0,252},{4,0},{8,4},{12,8},{16,12},{20,16},{24,20},{28,24},{32,28}... | collective-permute-start | bytes 589832 | tf_op jit(solution)/shard_map/ppermute | solution.py:12
  131.4 4.6 collective-permute-start.18
  137.4 4.7 collective-permute-start.27
  152.2 5.1 %collective-permute-start.24 = (f32[128]{0:T(128)S(1)}, f32[128]{0:T(128)S(1)}, u32[]{:S(2)}, u32[]{:S(2)}) collective-permute-start(f32[128]{0:T(128)S(1)} %get-tuple-element.19), channel_id=1, source_target_pairs={{0,16},{4,20},{8,24},{12,28},{16,32},{20,36},{24,40},{28,44},{32,4... | collective-permute-start | bytes 1544 | tf_op jit(solution)/shard_map/ppermute | solution.py:12
  182.7 5.1 %collective-permute-start.34 = (f32[128]{0:T(128)S(1)}, f32[128]{0:T(128)S(1)}, u32[]{:S(2)}, u32[]{:S(2)}) collective-permute-start(f32[128]{0:T(128)S(1)} %get-tuple-element.49), channel_id=1, source_target_pairs={{0,224},{4,228},{8,232},{12,236},{16,240},{20,244},{24,248},{28,25... | collective-permute-start | bytes 1544 | tf_op jit(solution)/shard_map/ppermute | solution.py:12
  197.9 6.1 %collective-permute-start.12 = (f32[128]{0:T(128)S(1)}, f32[128]{0:T(128)S(1)}, u32[]{:S(2)}, u32[]{:S(2)}) collective-permute-start(f32[128]{0:T(128)S(1)} %get-tuple-element.17), channel_id=1, source_target_pairs={{0,12},{4,16},{8,20},{12,24},{16,28},{20,32},{24,36},{28,40},{32,4... | collective-permute-start | bytes 1544 | tf_op jit(solution)/shard_map/ppermute | solution.py:12
  234.7 6.2 %collective-permute-start.51 = (f32[128]{0:T(128)S(1)}, f32[128]{0:T(128)S(1)}, u32[]{:S(2)}, u32[]{:S(2)}) collective-permute-start(f32[128]{0:T(128)S(1)} %get-tuple-element.36), channel_id=1, source_target_pairs={{0,160},{4,164},{8,168},{12,172},{16,176},{20,180},{24,184},{28,18... | collective-permute-start | bytes 1544 | tf_op jit(solution)/shard_map/ppermute | solution.py:12
  248.3 6.1 %collective-permute-start.53 = (f32[128]{0:T(128)S(1)}, f32[128]{0:T(128)S(1)}, u32[]{:S(2)}, u32[]{:S(2)}) collective-permute-start(f32[128]{0:T(128)S(1)} %get-tuple-element.36), channel_id=1, source_target_pairs={{0,96},{4,100},{8,104},{12,108},{16,112},{20,116},{24,120},{28,124... | collective-permute-start | bytes 1544 | tf_op jit(solution)/shard_map/ppermute | solution.py:12
  268.8 5.0 collective-permute-done.55
  286.3 6.4 %collective-permute-start.69 = (f32[128]{0:T(128)S(1)}, f32[128]{0:T(128)S(1)}, u32[]{:S(2)}, u32[]{:S(2)}) collective-permute-start(f32[128]{0:T(128)S(1)} %get-tuple-element.38), channel_id=1, source_target_pairs={{0,236},{4,240},{8,244},{12,248},{16,252},{20,0},{24,4},{28,8},{32... | collective-permute-start | bytes 1544 | tf_op jit(solution)/shard_map/ppermute | solution.py:12
  297.2 8.7 %collective-permute-start.75 = (f32[128]{0:T(128)S(1)}, f32[128]{0:T(128)S(1)}, u32[]{:S(2)}, u32[]{:S(2)}) collective-permute-start(f32[128]{0:T(128)S(1)} %get-tuple-element.38), channel_id=1, source_target_pairs={{0,228},{4,232},{8,236},{12,240},{16,244},{20,248},{24,252},{28,0}... | collective-permute-start | bytes 1544 | tf_op jit(solution)/shard_map/ppermute | solution.py:12
  332.7 32.8 %collective-permute-done.76 = f32[128,768]{1,0:T(8,128)} collective-permute-done((f32[128,768]{1,0:T(8,128)}, f32[128,768]{1,0:T(8,128)}, u32[]{:S(2)}, u32[]{:S(2)}) %collective-permute-start.76) | collective-permute-done | bytes 393248 | tf_op jit(solution)/shard_map/ppermute | solution.py:12
  366.8 9.1 %collective-permute-done.70 = f32[128,768]{1,0:T(8,128)} collective-permute-done((f32[128,768]{1,0:T(8,128)}, f32[128,768]{1,0:T(8,128)}, u32[]{:S(2)}, u32[]{:S(2)}) %collective-permute-start.70) | collective-permute-done | bytes 393248 | tf_op jit(solution)/shard_map/ppermute | solution.py:12
  379.2 11.9 %collective-permute-done.67 = f32[128,768]{1,0:T(8,128)} collective-permute-done((f32[128,768]{1,0:T(8,128)}, f32[128,768]{1,0:T(8,128)}, u32[]{:S(2)}, u32[]{:S(2)}) %collective-permute-start.67) | collective-permute-done | bytes 393248 | tf_op jit(solution)/shard_map/ppermute | solution.py:12
  391.1 6.0 %collective-permute-start.83 = (f32[128,768]{1,0:T(8,128)S(1)}, f32[128,768]{1,0:T(8,128)S(1)}, u32[]{:S(2)}, u32[]{:S(2)}) collective-permute-start(f32[128,768]{1,0:T(8,128)S(1)} %get-tuple-element.40), channel_id=1, source_target_pairs={{0,224},{4,228},{8,232},{12,236},{16,240},{20,244},{24,248},{28,25... | collective-permute-start | bytes 1179656 | tf_op jit(solution)/shard_map/ppermute | solution.py:12
  397.0 12.7 %collective-permute-done.64 = f32[128,768]{1,0:T(8,128)} collective-permute-done((f32[128,768]{1,0:T(8,128)}, f32[128,768]{1,0:T(8,128)}, u32[]{:S(2)}, u32[]{:S(2)}) %collective-permute-start.64) | collective-permute-done | bytes 393248 | tf_op jit(solution)/shard_map/ppermute | solution.py:12
  412.8 12.1 %collective-permute-done.61 = f32[128,768]{1,0:T(8,128)S(1)} collective-permute-done((f32[128,768]{1,0:T(8,128)S(1)}, f32[128,768]{1,0:T(8,128)S(1)}, u32[]{:S(2)}, u32[]{:S(2)}) %collective-permute-start.61) | collective-permute-done | bytes 393248 | tf_op jit(solution)/shard_map/ppermute | solution.py:12
  424.9 7.2 %collective-permute-start.81 = (f32[128,768]{1,0:T(8,128)S(1)}, f32[128,768]{1,0:T(8,128)S(1)}, u32[]{:S(2)}, u32[]{:S(2)}) collective-permute-start(f32[128,768]{1,0:T(8,128)S(1)} %get-tuple-element.42), channel_id=1, source_target_pairs={{0,160},{4,164},{8,168},{12,172},{16,176},{20,180},{24,184},{28,18... | collective-permute-start | bytes 1179656 | tf_op jit(solution)/shard_map/ppermute | solution.py:12
  432.0 50.6 %collective-permute-done.58 = f32[128,768]{1,0:T(8,128)S(1)} collective-permute-done((f32[128,768]{1,0:T(8,128)S(1)}, f32[128,768]{1,0:T(8,128)S(1)}, u32[]{:S(2)}, u32[]{:S(2)}) %collective-permute-start.58) | collective-permute-done | bytes 393248 | tf_op jit(solution)/shard_map/ppermute | solution.py:12
  492.0 4.8 collective-permute-done.79
  (225 shorter events, 205.1 us)
Async XLA Ops:
  1.9 146.4 %collective-permute-start.48 = (f32[128]{0:T(128)}, f32[128]{0:T(128)}, u32[]{:S(2)}, u32[]{:S(2)}) collective-permute-start(f32[128]{0:T(128)} %get-tuple-element.64), channel_id=1, source_target_pairs={{0,32},{4,36},{8,40},{12,44},{16,48},{20,52},{24,56},{28,60},{32,6... | collective-permute-start | bytes 1544 | tf_op jit(solution)/shard_map/ppermute | solution.py:12
  7.3 36.7 %collective-permute-start.47 = (f32[128]{0:T(128)}, f32[128]{0:T(128)S(1)}, u32[]{:S(2)}, u32[]{:S(2)}) collective-permute-start(f32[128]{0:T(128)} %get-tuple-element.64), channel_id=1, source_target_pairs={{0,64},{4,68},{8,72},{12,76},{16,80},{20,84},{24,88},{28,92},{32,9... | collective-permute-start | bytes 1544 | tf_op jit(solution)/shard_map/ppermute | solution.py:12
  8.8 32.7 %collective-permute-start.46 = (f32[128]{0:T(128)}, f32[128]{0:T(128)S(1)}, u32[]{:S(2)}, u32[]{:S(2)}) collective-permute-start(f32[128]{0:T(128)} %get-tuple-element.64), channel_id=1, source_target_pairs={{0,96},{4,100},{8,104},{12,108},{16,112},{20,116},{24,120},{28,124... | collective-permute-start | bytes 1544 | tf_op jit(solution)/shard_map/ppermute | solution.py:12
  10.9 29.7 %collective-permute-start.45 = (f32[128]{0:T(128)}, f32[128]{0:T(128)S(1)}, u32[]{:S(2)}, u32[]{:S(2)}) collective-permute-start(f32[128]{0:T(128)} %get-tuple-element.64), channel_id=1, source_target_pairs={{0,128},{4,132},{8,136},{12,140},{16,144},{20,148},{24,152},{28,15... | collective-permute-start | bytes 1544 | tf_op jit(solution)/shard_map/ppermute | solution.py:12
  35.2 57.2 %collective-permute-start.6 = (bf16[128,768]{1,0:T(8,128)(2,1)}, bf16[128,768]{1,0:T(8,128)(2,1)S(1)}, u32[]{:S(2)}, u32[]{:S(2)}) collective-permute-start(bf16[128,768]{1,0:T(8,128)(2,1)} %param.5), channel_id=1, source_target_pairs={{0,32},{4,36},{8,40},{12,44},{16,48},{20,52},{24,56},{28,60},{32,6... | collective-permute-start | bytes 589832 | tf_op jit(solution)/shard_map/ppermute | solution.py:12
  40.6 45.1 %collective-permute-start.5 = (bf16[128,768]{1,0:T(8,128)(2,1)}, bf16[128,768]{1,0:T(8,128)(2,1)S(1)}, u32[]{:S(2)}, u32[]{:S(2)}) collective-permute-start(bf16[128,768]{1,0:T(8,128)(2,1)} %param.5), channel_id=1, source_target_pairs={{0,64},{4,68},{8,72},{12,76},{16,80},{20,84},{24,88},{28,92},{32,9... | collective-permute-start | bytes 589832 | tf_op jit(solution)/shard_map/ppermute | solution.py:12
  84.7 27.6 %collective-permute-start.17 = (bf16[128,768]{1,0:T(8,128)(2,1)S(1)}, bf16[128,768]{1,0:T(8,128)(2,1)S(1)}, u32[]{:S(2)}, u32[]{:S(2)}) collective-permute-start(bf16[128,768]{1,0:T(8,128)(2,1)S(1)} %copy-done.2), channel_id=1, source_target_pairs={{0,232},{4,236},{8,240},{12,244},{16,248},{20,252},{24,0},{28,4},{... | collective-permute-start | bytes 589832 | tf_op jit(solution)/shard_map/ppermute | solution.py:12
  85.8 35.2 %collective-permute-start.15 = (bf16[128,768]{1,0:T(8,128)(2,1)S(1)}, bf16[128,768]{1,0:T(8,128)(2,1)S(1)}, u32[]{:S(2)}, u32[]{:S(2)}) collective-permute-start(bf16[128,768]{1,0:T(8,128)(2,1)S(1)} %copy-done.2), channel_id=1, source_target_pairs={{0,236},{4,240},{8,244},{12,248},{16,252},{20,0},{24,4},{28,8},{32... | collective-permute-start | bytes 589832 | tf_op jit(solution)/shard_map/ppermute | solution.py:12
  92.5 35.3 %collective-permute-start.13 = (bf16[128,768]{1,0:T(8,128)(2,1)S(1)}, bf16[128,768]{1,0:T(8,128)(2,1)S(1)}, u32[]{:S(2)}, u32[]{:S(2)}) collective-permute-start(bf16[128,768]{1,0:T(8,128)(2,1)S(1)} %copy-done.2), channel_id=1, source_target_pairs={{0,240},{4,244},{8,248},{12,252},{16,0},{20,4},{24,8},{28,12},{32,... | collective-permute-start | bytes 589832 | tf_op jit(solution)/shard_map/ppermute | solution.py:12
  99.4 32.1 %collective-permute-start.11 = (bf16[128,768]{1,0:T(8,128)(2,1)S(1)}, bf16[128,768]{1,0:T(8,128)(2,1)S(1)}, u32[]{:S(2)}, u32[]{:S(2)}) collective-permute-start(bf16[128,768]{1,0:T(8,128)(2,1)S(1)} %copy-done.2), channel_id=1, source_target_pairs={{0,244},{4,248},{8,252},{12,0},{16,4},{20,8},{24,12},{28,16},{32,2... | collective-permute-start | bytes 589832 | tf_op jit(solution)/shard_map/ppermute | solution.py:12
  112.4 25.1 %collective-permute-start.9 = (bf16[128,768]{1,0:T(8,128)(2,1)S(1)}, bf16[128,768]{1,0:T(8,128)(2,1)S(1)}, u32[]{:S(2)}, u32[]{:S(2)}) collective-permute-start(bf16[128,768]{1,0:T(8,128)(2,1)S(1)} %copy-done.2), channel_id=1, source_target_pairs={{0,248},{4,252},{8,0},{12,4},{16,8},{20,12},{24,16},{28,20},{32,24... | collective-permute-start | bytes 589832 | tf_op jit(solution)/shard_map/ppermute | solution.py:12
  121.0 22.5 %collective-permute-start.7 = (bf16[128,768]{1,0:T(8,128)(2,1)S(1)}, bf16[128,768]{1,0:T(8,128)(2,1)S(1)}, u32[]{:S(2)}, u32[]{:S(2)}) collective-permute-start(bf16[128,768]{1,0:T(8,128)(2,1)S(1)} %copy-done.2), channel_id=1, source_target_pairs={{0,252},{4,0},{8,4},{12,8},{16,12},{20,16},{24,20},{28,24},{32,28}... | collective-permute-start | bytes 589832 | tf_op jit(solution)/shard_map/ppermute | solution.py:12
  127.8 24.4 %collective-permute-start.20 = (f32[128]{0:T(128)S(1)}, f32[128]{0:T(128)S(1)}, u32[]{:S(2)}, u32[]{:S(2)}) collective-permute-start(f32[128]{0:T(128)S(1)} %get-tuple-element.33), channel_id=1, source_target_pairs={{0,28},{4,32},{8,36},{12,40},{16,44},{20,48},{24,52},{28,56},{32,6... | collective-permute-start | bytes 1544 | tf_op jit(solution)/shard_map/ppermute | solution.py:12
  131.4 25.9 %collective-permute-start.18 = (f32[128]{0:T(128)S(1)}, f32[128]{0:T(128)S(1)}, u32[]{:S(2)}, u32[]{:S(2)}) collective-permute-start(f32[128]{0:T(128)S(1)} %get-tuple-element.29), channel_id=1, source_target_pairs={{0,24},{4,28},{8,32},{12,36},{16,40},{20,44},{24,48},{28,52},{32,5... | collective-permute-start | bytes 1544 | tf_op jit(solution)/shard_map/ppermute | solution.py:12
  204.0 19.7 %collective-permute-start.8 = (f32[128]{0:T(128)S(1)}, f32[128]{0:T(128)S(1)}, u32[]{:S(2)}, u32[]{:S(2)}) collective-permute-start(f32[128]{0:T(128)S(1)} %get-tuple-element.9), channel_id=1, source_target_pairs={{0,4},{4,8},{8,12},{12,16},{16,20},{20,24},{24,28},{28,32},{32,36}... | collective-permute-start | bytes 1544 | tf_op jit(solution)/shard_map/ppermute | solution.py:12
  210.8 97.6 %collective-permute-start.74 = (f32[128]{0:T(128)S(1)}, f32[128]{0:T(128)S(1)}, u32[]{:S(2)}, u32[]{:S(2)}) collective-permute-start(f32[128]{0:T(128)S(1)} %get-tuple-element.65), channel_id=1, source_target_pairs={{0,228},{4,232},{8,236},{12,240},{16,244},{20,248},{24,252},{28,0}... | collective-permute-start | bytes 1544 | tf_op jit(solution)/shard_map/ppermute | solution.py:12
  214.1 60.5 %collective-permute-start.71 = (f32[128]{0:T(128)S(1)}, f32[128]{0:T(128)S(1)}, u32[]{:S(2)}, u32[]{:S(2)}) collective-permute-start(f32[128]{0:T(128)S(1)} %get-tuple-element.65), channel_id=1, source_target_pairs={{0,232},{4,236},{8,240},{12,244},{16,248},{20,252},{24,0},{28,4},{... | collective-permute-start | bytes 1544 | tf_op jit(solution)/shard_map/ppermute | solution.py:12
  217.9 77.3 %collective-permute-start.68 = (f32[128]{0:T(128)S(1)}, f32[128]{0:T(128)S(1)}, u32[]{:S(2)}, u32[]{:S(2)}) collective-permute-start(f32[128]{0:T(128)S(1)} %get-tuple-element.65), channel_id=1, source_target_pairs={{0,236},{4,240},{8,244},{12,248},{16,252},{20,0},{24,4},{28,8},{32... | collective-permute-start | bytes 1544 | tf_op jit(solution)/shard_map/ppermute | solution.py:12
  220.5 89.9 %collective-permute-start.65 = (f32[128]{0:T(128)S(1)}, f32[128]{0:T(128)S(1)}, u32[]{:S(2)}, u32[]{:S(2)}) collective-permute-start(f32[128]{0:T(128)S(1)} %get-tuple-element.65), channel_id=1, source_target_pairs={{0,240},{4,244},{8,248},{12,252},{16,0},{20,4},{24,8},{28,12},{32,... | collective-permute-start | bytes 1544 | tf_op jit(solution)/shard_map/ppermute | solution.py:12
  281.1 40.1 %collective-permute-start.59 = (f32[128]{0:T(128)S(1)}, f32[128]{0:T(128)S(1)}, u32[]{:S(2)}, u32[]{:S(2)}) collective-permute-start(f32[128]{0:T(128)S(1)} %get-tuple-element.65), channel_id=1, source_target_pairs={{0,248},{4,252},{8,0},{12,4},{16,8},{20,12},{24,16},{28,20},{32,24... | collective-permute-start | bytes 1544 | tf_op jit(solution)/shard_map/ppermute | solution.py:12
  295.2 33.1 %collective-permute-start.56 = (f32[128]{0:T(128)S(1)}, f32[128]{0:T(128)S(1)}, u32[]{:S(2)}, u32[]{:S(2)}) collective-permute-start(f32[128]{0:T(128)S(1)} %get-tuple-element.65), channel_id=1, source_target_pairs={{0,252},{4,0},{8,4},{12,8},{16,12},{20,16},{24,20},{28,24},{32,28}... | collective-permute-start | bytes 1544 | tf_op jit(solution)/shard_map/ppermute | solution.py:12
  314.3 51.3 %collective-permute-start.76 = (f32[128,768]{1,0:T(8,128)}, f32[128,768]{1,0:T(8,128)}, u32[]{:S(2)}, u32[]{:S(2)}) collective-permute-start(f32[128,768]{1,0:T(8,128)} %fusion.86), channel_id=1, source_target_pairs={{0,28},{4,32},{8,36},{12,40},{16,44},{20,48},{24,52},{28,56},{32,6... | collective-permute-start | bytes 1179656 | tf_op jit(solution)/shard_map/ppermute | solution.py:12
  321.2 45.5 %collective-permute-start.73 = (f32[128,768]{1,0:T(8,128)}, f32[128,768]{1,0:T(8,128)}, u32[]{:S(2)}, u32[]{:S(2)}) collective-permute-start(f32[128,768]{1,0:T(8,128)} %fusion.84), channel_id=1, source_target_pairs={{0,24},{4,28},{8,32},{12,36},{16,40},{20,44},{24,48},{28,52},{32,5... | collective-permute-start | bytes 1179656 | tf_op jit(solution)/shard_map/ppermute | solution.py:12
  322.8 53.1 %collective-permute-start.70 = (f32[128,768]{1,0:T(8,128)}, f32[128,768]{1,0:T(8,128)}, u32[]{:S(2)}, u32[]{:S(2)}) collective-permute-start(f32[128,768]{1,0:T(8,128)} %fusion.82), channel_id=1, source_target_pairs={{0,20},{4,24},{8,28},{12,32},{16,36},{20,40},{24,44},{28,48},{32,5... | collective-permute-start | bytes 1179656 | tf_op jit(solution)/shard_map/ppermute | solution.py:12
  328.3 62.8 %collective-permute-start.67 = (f32[128,768]{1,0:T(8,128)}, f32[128,768]{1,0:T(8,128)}, u32[]{:S(2)}, u32[]{:S(2)}) collective-permute-start(f32[128,768]{1,0:T(8,128)} %fusion.80), channel_id=1, source_target_pairs={{0,16},{4,20},{8,24},{12,28},{16,32},{20,36},{24,40},{28,44},{32,4... | collective-permute-start | bytes 1179656 | tf_op jit(solution)/shard_map/ppermute | solution.py:12
  328.3 81.4 %collective-permute-start.64 = (f32[128,768]{1,0:T(8,128)}, f32[128,768]{1,0:T(8,128)}, u32[]{:S(2)}, u32[]{:S(2)}) collective-permute-start(f32[128,768]{1,0:T(8,128)} %fusion.78), channel_id=1, source_target_pairs={{0,12},{4,16},{8,20},{12,24},{16,28},{20,32},{24,36},{28,40},{32,4... | collective-permute-start | bytes 1179656 | tf_op jit(solution)/shard_map/ppermute | solution.py:12
  365.5 59.3 %collective-permute-start.61 = (f32[128,768]{1,0:T(8,128)S(1)}, f32[128,768]{1,0:T(8,128)S(1)}, u32[]{:S(2)}, u32[]{:S(2)}) collective-permute-start(f32[128,768]{1,0:T(8,128)S(1)} %fusion.76), channel_id=1, source_target_pairs={{0,8},{4,12},{8,16},{12,20},{16,24},{20,28},{24,32},{28,36},{32,40... | collective-permute-start | bytes 1179656 | tf_op jit(solution)/shard_map/ppermute | solution.py:12
  366.7 115.9 %collective-permute-start.58 = (f32[128,768]{1,0:T(8,128)S(1)}, f32[128,768]{1,0:T(8,128)S(1)}, u32[]{:S(2)}, u32[]{:S(2)}) collective-permute-start(f32[128,768]{1,0:T(8,128)S(1)} %fusion.74), channel_id=1, source_target_pairs={{0,4},{4,8},{8,12},{12,16},{16,20},{20,24},{24,28},{28,32},{32,36}... | collective-permute-start | bytes 1179656 | tf_op jit(solution)/shard_map/ppermute | solution.py:12
  375.9 106.7 %collective-permute-start.77 = (f32[128,768]{1,0:T(8,128)S(1)}, f32[128,768]{1,0:T(8,128)S(1)}, u32[]{:S(2)}, u32[]{:S(2)}) collective-permute-start(f32[128,768]{1,0:T(8,128)S(1)} %get-tuple-element.39), channel_id=1, source_target_pairs={{0,32},{4,36},{8,40},{12,44},{16,48},{20,52},{24,56},{28,60},{32,6... | collective-permute-start | bytes 1179656 | tf_op jit(solution)/shard_map/ppermute | solution.py:12
  391.1 92.6 %collective-permute-start.83 = (f32[128,768]{1,0:T(8,128)S(1)}, f32[128,768]{1,0:T(8,128)S(1)}, u32[]{:S(2)}, u32[]{:S(2)}) collective-permute-start(f32[128,768]{1,0:T(8,128)S(1)} %get-tuple-element.40), channel_id=1, source_target_pairs={{0,224},{4,228},{8,232},{12,236},{16,240},{20,244},{24,248},{28,25... | collective-permute-start | bytes 1179656 | tf_op jit(solution)/shard_map/ppermute | solution.py:12
  409.7 77.7 %collective-permute-start.82 = (f32[128,768]{1,0:T(8,128)S(1)}, f32[128,768]{1,0:T(8,128)S(1)}, u32[]{:S(2)}, u32[]{:S(2)}) collective-permute-start(f32[128,768]{1,0:T(8,128)S(1)} %get-tuple-element.41), channel_id=1, source_target_pairs={{0,192},{4,196},{8,200},{12,204},{16,208},{20,212},{24,216},{28,22... | collective-permute-start | bytes 1179656 | tf_op jit(solution)/shard_map/ppermute | solution.py:12
  424.9 62.6 %collective-permute-start.81 = (f32[128,768]{1,0:T(8,128)S(1)}, f32[128,768]{1,0:T(8,128)S(1)}, u32[]{:S(2)}, u32[]{:S(2)}) collective-permute-start(f32[128,768]{1,0:T(8,128)S(1)} %get-tuple-element.42), channel_id=1, source_target_pairs={{0,160},{4,164},{8,168},{12,172},{16,176},{20,180},{24,184},{28,18... | collective-permute-start | bytes 1179656 | tf_op jit(solution)/shard_map/ppermute | solution.py:12
  (63 other events, 1403.9 us)
where the time goes:
time: 511 us; the launch traced here: 502 us
  starting transfers between devices  252 us (49%)
  waiting for transfers between devices  211 us (41%)
  matrix products  25 us (5%)
  other arithmetic  7.56 us (1%)
    ppermute x84, starting transfers between devices, shifted(): return lax.ppermute(value, axis, pairs)  252 us
    ppermute x84, waiting for transfers between devices, shifted(): return lax.ppermute(value, axis, pairs)  211 us
    dot_general x8, matrix products, dot_lead(): lax.dot_general(left, right, (((0,), (0,)), ((), ())), preferred_element_...  13.3 us
  transfers between devices with their start and end apart: 84, of which 29 were waited for; matrix products, arithmetic and copies ran while one was open for 7% of the time, Pallas kernels for 0%

commit v1 on v0

v1 whole, which is shorter than its diff:
```python
import jax
import jax.numpy as jnp
from jax import lax
from jax.sharding import Mesh, PartitionSpec as P

ROWS = "z"
COLS = ("x", "h")


def spread(value, axis):
    copies = jnp.broadcast_to(value[None], (lax.axis_size(axis),) + value.shape)
    return lax.all_to_all(copies, axis, 0, 0, tiled=True)


def merge_lse(parts):
    top = jnp.max(parts, axis=0)
    return top + jnp.log(jnp.sum(jnp.exp(parts - top[None]), axis=0))


def shards(images, texts, scale, cotangent):
    n = images.shape[0]
    width = images.shape[1]
    logit_scale = scale[0]
    row_n = lax.axis_size(ROWS)
    col_n = lax.axis_size(COLS)
    img = spread(images, ROWS).reshape(row_n * n, width)
    txt = spread(texts, COLS).reshape(col_n * n, width)
    scores = logit_scale * lax.dot_general(
        img, txt, (((1,), (1,)), ((), ())), preferred_element_type=jnp.float32
    )
    row_top = jnp.max(scores, axis=1)
    row_part = row_top + jnp.log(jnp.sum(jnp.exp(scores - row_top[:, None]), axis=1))
    col_top = jnp.max(scores, axis=0)
    col_part = col_top + jnp.log(jnp.sum(jnp.exp(scores - col_top[None, :]), axis=0))
    row_msg = jnp.concatenate([row_part.reshape(row_n, n), cotangent[:1]], axis=0)
    col_msg = jnp.concatenate([col_part.reshape(col_n, n), cotangent[1:]], axis=0)
    row_all = spread(row_msg, ROWS)
    col_all = spread(col_msg, COLS)
    row_lse = merge_lse(row_all[:, :row_n])
    col_lse = merge_lse(col_all[:, :col_n])
    row_cot = row_all[:, row_n].reshape(-1)
    col_cot = col_all[:, col_n].reshape(-1)
    weights = row_cot[:, None] * jnp.exp(scores - row_lse.reshape(-1)[:, None]) + col_cot[
        None, :
    ] * jnp.exp(scores - col_lse.reshape(-1)[None, :])
    weights = weights.astype(jnp.bfloat16)
    img_part = jnp.dot(weights, txt, preferred_element_type=jnp.float32).astype(jnp.bfloat16)
    txt_part = lax.dot_general(
        weights, img, (((0,), (0,)), ((), ())), preferred_element_type=jnp.float32
    ).astype(jnp.bfloat16)
    img_sent = lax.all_to_all(img_part.reshape(row_n, n, width), ROWS, 0, 0, tiled=True)
    txt_sent = lax.all_to_all(txt_part.reshape(col_n, n, width), COLS, 0, 0, tiled=True)
    wide_i = images.astype(jnp.float32)
    wide_t = texts.astype(jnp.float32)
    matched = logit_scale * jnp.sum(wide_i * wide_t, axis=1)
    own_row = lax.dynamic_index_in_dim(row_lse, lax.axis_index(ROWS), 0, keepdims=False)
    own_col = lax.dynamic_index_in_dim(col_lse, lax.axis_index(COLS), 0, keepdims=False)
    row_losses = jnp.stack([own_row - matched, own_col - matched])
    both_cot = (cotangent[0] + cotangent[1])[:, None]
    grad_images = logit_scale * (
        jnp.sum(img_sent.astype(jnp.float32), axis=0) - both_cot * wide_t
    )
    grad_texts = logit_scale * (
        jnp.sum(txt_sent.astype(jnp.float32), axis=0) - both_cot * wide_i
    )
    return (row_losses, grad_images, grad_texts)


def solution(mesh):
    grid = Mesh(mesh.devices.reshape(4, 8, 2, 4), ("x", "z", "h", "dp"))
    rows = ("dp", "x", "z", "h")
    return jax.shard_map(
        shards,
        mesh=grid,
        in_specs=(P(rows, None), P(rows, None), P(), P(None, rows)),
        out_specs=(P(None, rows), P(rows, None), P(rows, None)),
        check_vma=False,
    )
```

time: 511 us -> 184 us (0.36)
  the two profiles are of different devices: /device:TPU:64 before, /device:TPU:1 now
where the time goes in v1:
time: 184 us
  waiting for transfers between devices  110 us (60%)
  blocking collectives  28.3 us (15%)
  starting transfers between devices  22.3 us (12%)
  matrix products  9.51 us (5%)
  other arithmetic  8.39 us (5%)
  local copies, waits for them, and re-layouts  3.79 us (2%)
    all_to_all x3, waiting for transfers between devices, spread(): return lax.all_to_all(copies, axis, 0, 0, tiled=True)  53.5 us
    all_to_all x1, waiting for transfers between devices, shards(): lax.all_to_all(img_part.reshape(row_n, n, width), ROWS, 0, 0, tiled=True)  40.1 us
    all_to_all x1, blocking collectives, spread(): return lax.all_to_all(copies, axis, 0, 0, tiled=True)  28.3 us
    all_to_all x1, waiting for transfers between devices, shards(): lax.all_to_all(txt_part.reshape(col_n, n, width), COLS, 0, 0, tiled=True)  16.3 us
    all_to_all x3, starting transfers between devices, spread(): return lax.all_to_all(copies, axis, 0, 0, tiled=True)  15.1 us
    dot_general x1, matrix products, shards(): jnp.dot(weights, txt, preferred_element_type=jnp.float32)  4.57 us
  transfers between devices with their start and end apart: 5, of which 5 were waited for; matrix products, arithmetic and copies ran while one was open for 3% of the time, Pallas kernels for 0%

profile of v1, /device:TPU:1, one launch (start us, length us, event | category | flops | bytes accessed | tf_op | source)
XLA Modules:
  0.0 183.6 jit_solution(15712927381709552892)
XLA Ops:
  0.6 0.0 copy-start.2
  0.6 1.1 broadcast_in_dim.9
  1.7 28.3 %all_to_all.30 = bf16[8,128,768]{2,1,0:T(8,128)(2,1)S(1)} all-to-all(bf16[8,128,768]{2,1,0:T(8,128)(2,1)S(1)} %broadcast_in_dim.9), channel_id=1, replica_groups=mesh['x'=4,'z'=8,'h'=2,'dp'=4] {'x','h'}, dimensions={0} | all-to-all | bytes 3145728 | tf_op jit(solution)/shard_map/all_to_all | solution.py:12
  30.0 0.0 copy-done.2
  30.0 0.0 copy-start.3
  30.0 1.3 broadcast_in_dim.8
  31.2 8.2 %all-to-all-start = ((bf16[8,128,768]{2,1,0:T(8,128)(2,1)}), bf16[8,128,768]{2,1,0:T(8,128)(2,1)S(1)}, u32[]{:S(2)}, u32[]{:S(2)}) async-start(bf16[8,128,768]{2,1,0:T(8,128)(2,1)} %broadcast_in_dim.8), calls=%async_computation | async-start | bytes 3145728 | tf_op jit(solution)/shard_map/all_to_all | solution.py:12
  40.1 0.0 copy-done.3
  40.1 39.8 %all-to-all-done = bf16[8,128,768]{2,1,0:T(8,128)(2,1)S(1)} async-done(((bf16[8,128,768]{2,1,0:T(8,128)(2,1)}), bf16[8,128,768]{2,1,0:T(8,128)(2,1)S(1)}, u32[]{:S(2)}, u32[]{:S(2)}) %all-to-all-start) | async-done | bytes 1572896 | tf_op jit(solution)/shard_map/all_to_all | solution.py:12
  79.9 1.9 %multiply_reduce_fusion.1 = (f32[1024]{0:T(1024)S(1)}, f32[1024,1024]{1,0:T(8,128)S(1)}) fusion(f32[]{:T(128)} %bitcast.24, bf16[1024,768]{1,0:T(8,128)(2,1)S(1)} %bitcast.32, bf16[1024,768]{1,0:T(8,128)(2,1)S(1)} %bitcast.30), kind=kOutput, calls=%fused_computation.4 | convolution fusion | flops 1612708864 | bytes 7344132 | tf_op jit(solution)/shard_map/dot_general | solution.py:28
  81.8 1.0 exponential_reduce_fusion.1
  82.8 0.7 exponential_reduce_fusion
  83.5 0.2 copy-done
  83.7 0.6 broadcast_in_dim.11
  84.3 3.6 %all-to-all-start.3 = ((f32[8,9,128]{2,1,0:T(8,128)}), f32[8,9,128]{2,1,0:T(8,128)S(1)}, u32[]{:S(2)}, u32[]{:S(2)}) async-start(f32[8,9,128]{2,1,0:T(8,128)} %broadcast_in_dim.11), calls=%async_computation.3 | async-start | bytes 131072 | tf_op jit(solution)/shard_map/all_to_all | solution.py:12
  88.0 6.6 %all-to-all-done.3 = f32[8,9,128]{2,1,0:T(8,128)S(1)} async-done(((f32[8,9,128]{2,1,0:T(8,128)}), f32[8,9,128]{2,1,0:T(8,128)S(1)}, u32[]{:S(2)}, u32[]{:S(2)}) %all-to-all-start.3) | async-done | bytes 36896 | tf_op jit(solution)/shard_map/all_to_all | solution.py:12
  94.6 0.6 broadcast_in_dim.10
  95.2 3.4 %all-to-all-start.2 = ((f32[8,9,128]{2,1,0:T(8,128)}), f32[8,9,128]{2,1,0:T(8,128)S(1)}, u32[]{:S(2)}, u32[]{:S(2)}) async-start(f32[8,9,128]{2,1,0:T(8,128)} %broadcast_in_dim.10), calls=%async_computation.2 | async-start | bytes 131072 | tf_op jit(solution)/shard_map/all_to_all | solution.py:12
  98.6 7.2 %all-to-all-done.2 = f32[8,9,128]{2,1,0:T(8,128)S(1)} async-done(((f32[8,9,128]{2,1,0:T(8,128)}), f32[8,9,128]{2,1,0:T(8,128)S(1)}, u32[]{:S(2)}, u32[]{:S(2)}) %all-to-all-start.2) | async-done | bytes 36896 | tf_op jit(solution)/shard_map/all_to_all | solution.py:12
  105.9 3.4 %add_convert_fusion = bf16[1024,1024]{1,0:T(8,128)(2,1)S(1)} fusion(f32[1024,1024]{1,0:T(8,128)} %copy-done, f32[1024]{0:T(1024)S(1)} %bitcast.36, f32[1024]{0:T(1024)S(1)} %bitcast.38, f32[1024]{0:T(1024)S(1)} %bitcast.37, f32[1024]{0:T(1024)S(1)} %bitcast.39, f32[]{:T(128)} %bitcast.28), kind=kLoop, calls=%fused_computation | loop fusion | flops 7340032 | bytes 6307844 | tf_op jit(solution)/shard_map/convert_element_type | solution.py:46
  109.3 0.0 copy-start.1
  109.3 3.0 %convolution_convert_fusion = bf16[1024,768]{1,0:T(8,128)(2,1)} fusion(bf16[1024,1024]{1,0:T(8,128)(2,1)S(1)} %add_convert_fusion, bf16[1024,768]{1,0:T(8,128)(2,1)S(1)} %bitcast.33), kind=kOutput, calls=%fused_computation.7 | convolution fusion | flops 1611399168 | bytes 5242880 | tf_op jit(solution)/shard_map/dot_general | solution.py:48
  112.4 0.0 copy-done.1
  112.4 3.6 %all-to-all-start.5 = ((bf16[8,128,768]{2,1,0:T(8,128)(2,1)}), bf16[8,128,768]{2,1,0:T(8,128)(2,1)S(1)}, u32[]{:S(2)}, u32[]{:S(2)}) async-start(bf16[8,128,768]{2,1,0:T(8,128)(2,1)} %bitcast.35), calls=%async_computation.5 | async-start | bytes 3145728 | tf_op jit(solution)/shard_map/all_to_all | solution.py:52
  116.0 4.6 %convolution_convert_fusion.1 = bf16[1024,768]{1,0:T(8,128)(2,1)} fusion(bf16[1024,1024]{1,0:T(8,128)(2,1)} %copy-done.1, bf16[1024,768]{1,0:T(8,128)(2,1)S(1)} %bitcast.31), kind=kOutput, calls=%fused_computation.8 | convolution fusion | flops 1611399168 | bytes 5242880 | tf_op jit(solution)/shard_map/dot_general | solution.py:47
  120.5 16.3 %all-to-all-done.5 = bf16[8,128,768]{2,1,0:T(8,128)(2,1)S(1)} async-done(((bf16[8,128,768]{2,1,0:T(8,128)(2,1)}), bf16[8,128,768]{2,1,0:T(8,128)(2,1)S(1)}, u32[]{:S(2)}, u32[]{:S(2)}) %all-to-all-start.5) | async-done | bytes 1572896 | tf_op jit(solution)/shard_map/all_to_all | solution.py:52
  136.8 3.6 %all-to-all-start.4 = ((bf16[8,128,768]{2,1,0:T(8,128)(2,1)}), bf16[8,128,768]{2,1,0:T(8,128)(2,1)S(1)}, u32[]{:S(2)}, u32[]{:S(2)}) async-start(bf16[8,128,768]{2,1,0:T(8,128)(2,1)} %bitcast.34), calls=%async_computation.4 | async-start | bytes 3145728 | tf_op jit(solution)/shard_map/all_to_all | solution.py:51
  140.4 0.2 convert_reduce_fusion
  140.6 40.1 %all-to-all-done.4 = bf16[8,128,768]{2,1,0:T(8,128)(2,1)S(1)} async-done(((bf16[8,128,768]{2,1,0:T(8,128)(2,1)}), bf16[8,128,768]{2,1,0:T(8,128)(2,1)S(1)}, u32[]{:S(2)}, u32[]{:S(2)}) %all-to-all-start.4) | async-done | bytes 1572896 | tf_op jit(solution)/shard_map/all_to_all | solution.py:51
  180.7 0.2 convert_reduce_fusion.1
  181.0 2.1 %fusion.1 = (f32[128,768]{1,0:T(8,128)}, f32[128]{0:T(128)S(1)}, f32[128,768]{1,0:T(8,128)}) fusion(f32[128,768]{1,0:T(8,128)S(1)} %convert_reduce_fusion, bf16[128,768]{1,0:T(8,128)(2,1)} %param.4, f32[128]{0:T(128)S(1)} %get-tuple-element.8, f32[]{:T(128)} %bitcast.26, bf16[128,768]{1,0:T(8,128)(2,1)} %param.5, f32[128,768]{1,0:T(8,128)S(1)} %convert_reduce_fusion.1), kind=kLoop, calls=%fused_computation.13 | loop fusion | flops 982912 | bytes 1967108 | tf_op jit(solution)/shard_map/mul | solution.py:63
  183.1 0.6 pad_maximum_fusion.2
  (14 shorter events, 0.1 us)
Async XLA Ops:
  0.6 29.3 %copy-start.2 = (bf16[128,768]{1,0:T(8,128)(2,1)S(1)}, bf16[128,768]{1,0:T(8,128)(2,1)}, u32[]{:S(2)}) copy-start(bf16[128,768]{1,0:T(8,128)(2,1)} %param.4) | copy-start | bytes 589828
  30.0 10.1 %copy-start.3 = (f32[2,128]{1,0:T(2,128)S(1)}, f32[2,128]{1,0:T(2,128)}, u32[]{:S(2)}) copy-start(f32[2,128]{1,0:T(2,128)} %param.7) | copy-start | bytes 3076
  31.2 48.6 %all-to-all-start = ((bf16[8,128,768]{2,1,0:T(8,128)(2,1)}), bf16[8,128,768]{2,1,0:T(8,128)(2,1)S(1)}, u32[]{:S(2)}, u32[]{:S(2)}) async-start(bf16[8,128,768]{2,1,0:T(8,128)(2,1)} %broadcast_in_dim.8), calls=%async_computation | async-start | bytes 3145728 | tf_op jit(solution)/shard_map/all_to_all | solution.py:12
  81.8 1.9 %copy-start = (f32[1024,1024]{1,0:T(8,128)}, f32[1024,1024]{1,0:T(8,128)S(1)}, u32[]{:S(2)}) copy-start(f32[1024,1024]{1,0:T(8,128)S(1)} %get-tuple-element.14) | copy-start | bytes 12582916
  84.3 10.2 %all-to-all-start.3 = ((f32[8,9,128]{2,1,0:T(8,128)}), f32[8,9,128]{2,1,0:T(8,128)S(1)}, u32[]{:S(2)}, u32[]{:S(2)}) async-start(f32[8,9,128]{2,1,0:T(8,128)} %broadcast_in_dim.11), calls=%async_computation.3 | async-start | bytes 131072 | tf_op jit(solution)/shard_map/all_to_all | solution.py:12
  95.2 10.6 %all-to-all-start.2 = ((f32[8,9,128]{2,1,0:T(8,128)}), f32[8,9,128]{2,1,0:T(8,128)S(1)}, u32[]{:S(2)}, u32[]{:S(2)}) async-start(f32[8,9,128]{2,1,0:T(8,128)} %broadcast_in_dim.10), calls=%async_computation.2 | async-start | bytes 131072 | tf_op jit(solution)/shard_map/all_to_all | solution.py:12
  109.3 3.1 %copy-start.1 = (bf16[1024,1024]{1,0:T(8,128)(2,1)}, bf16[1024,1024]{1,0:T(8,128)(2,1)S(1)}, u32[]{:S(2)}) copy-start(bf16[1024,1024]{1,0:T(8,128)(2,1)S(1)} %add_convert_fusion) | copy-start | bytes 6291460
  112.4 24.5 %all-to-all-start.5 = ((bf16[8,128,768]{2,1,0:T(8,128)(2,1)}), bf16[8,128,768]{2,1,0:T(8,128)(2,1)S(1)}, u32[]{:S(2)}, u32[]{:S(2)}) async-start(bf16[8,128,768]{2,1,0:T(8,128)(2,1)} %bitcast.35), calls=%async_computation.5 | async-start | bytes 3145728 | tf_op jit(solution)/shard_map/all_to_all | solution.py:52
  136.8 43.9 %all-to-all-start.4 = ((bf16[8,128,768]{2,1,0:T(8,128)(2,1)}), bf16[8,128,768]{2,1,0:T(8,128)(2,1)S(1)}, u32[]{:S(2)}, u32[]{:S(2)}) async-start(bf16[8,128,768]{2,1,0:T(8,128)(2,1)} %bitcast.34), calls=%async_computation.4 | async-start | bytes 3145728 | tf_op jit(solution)/shard_map/all_to_all | solution.py:51
